TPU v7x, 32 devices: a whole 2x2x4 slice. The times are simulated.
32 devices in a mesh: rows: 4 (over z), cx: 2 (over y), cy: 4 (over x, core).
Axes of the slice: x: 2, y: 2, z: 4, core: 2. Of those that a mesh axis runs over, the one named last changes fastest.
Arguments:
- rows_data: float32 [2048, 1024], P(('rows', 'cx', 'cy')), may hold values from -6 to 6
- owner_rows: int32 [2048, 1], P(('rows', 'cx', 'cy')), may hold values from 0 to 7; in each aligned block of 64 rows (0 to 63, 64 to 127, ...) at most 16 rows name the same one
- slot_rows: int32 [2048], P(('rows', 'cx', 'cy')), may hold values from 0 to 2047
- centroids: float32 [16384, 1024], P(('cx', 'cy'), 'rows'), may hold values from -6 to 6
- counts: float32 [16384], P(('cx', 'cy')), may hold values from 1 to 100
- owner_cent: int32 [16384, 1], P(('cx', 'cy')), may hold values from 0 to 7; in each aligned block of 2048 rows (0 to 2047, 2048 to 4095, ...) at most 512 rows name the same one
- slot_cent: int32 [16384], P(('cx', 'cy')), may hold values from 0 to 511
- upper: float32 [4096, 1024], P(('cx', 'cy'), 'rows'), may hold values from -6 to 6
- upper_counts: float32 [4096], P(('cx', 'cy')), may hold values from 1 to 100
Outputs:
- moved: float32 [16384, 1024], P(('cx', 'cy'), 'rows')
- new_counts: float32 [16384], P(('cx', 'cy'))
- new_upper: float32 [4096, 1024], P(('cx', 'cy'), 'rows')
- new_upper_counts: float32 [4096], P(('cx', 'cy'))
Inputs may be any that keep to these rules, and one draw needn't show every extreme that they name: `owner_rows`: the rows of one device name each value at most 16 times, and some device reaches it. `owner_cent`: the 2048 level-1 centroids of one shard name each value at most 512 times, and some shard reaches it.
All inputs are finite; a program needn't handle non-finite values.
Results may differ from a plain program's by a relative error of at most 0.00002.
Values sent between devices are 32-bit elements; how exact they have to be, the bound alone decides.
A program may use at most 64 MiB of HBM per device.

v0:
```python
import jax
import jax.numpy as jnp
from jax import lax
from jax.sharding import PartitionSpec as P


def bucket(values, owners, slot_ids, shards, capacity, empty):
    onehot = (owners[:, None] == jnp.arange(shards, dtype=jnp.int32)[None, :]).astype(jnp.int32)
    earlier = jnp.cumsum(onehot, axis=0) - onehot
    position = jnp.sum(earlier * onehot, axis=1)
    target = owners * capacity + position
    buffer = jnp.zeros((shards * capacity, values.shape[1]), values.dtype).at[target].set(values)
    labels = jnp.full((shards * capacity,), empty, jnp.int32).at[target].set(slot_ids)
    return (buffer.reshape(shards, capacity, values.shape[1]), labels.reshape(shards, capacity))


def accumulate(values, labels, segments):
    summed = jnp.zeros((segments, values.shape[1]), jnp.float32).at[labels].add(values, mode="drop")
    member_counts = (
        jnp.zeros((segments,), jnp.float32)
        .at[labels]
        .add(jnp.ones(labels.shape, jnp.float32), mode="drop")
    )
    return (summed, member_counts)


def damped(previous, weights, summed, member_counts):
    denominator = weights + member_counts
    updated = previous + (summed - member_counts[:, None] * previous) / denominator[:, None]
    return (updated, denominator)


def body(
    rows_data, owner_rows, slot_rows, centroids, counts, owner_cent, slot_cent, upper, upper_counts
):
    shards = lax.axis_size(("cx", "cy"))
    groups = lax.axis_size("rows")
    batch = rows_data.shape[0]
    lower_rows = centroids.shape[0]
    capacity = 2 * batch // shards
    buffer, labels = bucket(rows_data, owner_rows[:, 0], slot_rows, shards, capacity, lower_rows)
    labels = jnp.broadcast_to(labels[:, :, None], (shards, capacity, groups))
    arrived, arrived_labels = (
        lax.all_to_all(
            lax.all_to_all(buffer, "rows", split_axis=2, concat_axis=1, tiled=True),
            ("cx", "cy"),
            split_axis=0,
            concat_axis=0,
            tiled=True,
        ),
        lax.all_to_all(
            lax.all_to_all(labels, "rows", split_axis=2, concat_axis=1, tiled=True),
            ("cx", "cy"),
            split_axis=0,
            concat_axis=0,
            tiled=True,
        ),
    )
    slice_width = arrived.shape[2]
    summed, member_counts = accumulate(
        arrived.reshape(-1, slice_width), arrived_labels.reshape(-1), lower_rows
    )
    moved, new_counts = damped(centroids, counts, summed, member_counts)
    upper_rows = upper.shape[0]
    owners_upper = owner_cent[:, 0]
    labels_upper = owners_upper * upper_rows + slot_cent
    whole_partial, hit_counts = accumulate(moved, labels_upper, upper_rows * shards)
    upper_summed = lax.psum_scatter(whole_partial, ("cx", "cy"), scatter_dimension=0, tiled=True)
    upper_members = lax.psum_scatter(hit_counts, ("cx", "cy"), scatter_dimension=0, tiled=True)
    new_upper, new_upper_counts = damped(upper, upper_counts, upper_summed, upper_members)
    return (moved, new_counts, new_upper, new_upper_counts)


def solution(mesh):
    placed = (
        P(("rows", "cx", "cy"), None),
        P(("rows", "cx", "cy"), None),
        P(("rows", "cx", "cy")),
        P(("cx", "cy"), "rows"),
        P(("cx", "cy")),
        P(("cx", "cy"), None),
        P(("cx", "cy")),
        P(("cx", "cy"), "rows"),
        P(("cx", "cy")),
    )
    return jax.shard_map(
        body,
        mesh=mesh,
        in_specs=placed,
        out_specs=(
            P(("cx", "cy"), "rows"),
            P(("cx", "cy")),
            P(("cx", "cy"), "rows"),
            P(("cx", "cy")),
        ),
        check_vma=False,
    )
```

profile of v0, /device:TPU:0, one launch (start us, length us, event | category | flops | bytes accessed | tf_op | source)
XLA Modules:
  0.0 151.4 jit_solution(6357609695715163591)
XLA Ops:
  7.2 0.7 fusion.6
  8.0 0.8 select_reduce_fusion
  8.8 0.7 fusion.11
  9.5 0.9 scatter_custom_fusion
  10.5 0.7 reshape.128
  11.2 6.3 %all-to-all-start = ((s32[4,1,128]{2,1,0:T(1,128)}), s32[4,1,128]{2,1,0:T(1,128)S(1)}, u32[]{:S(2)}, u32[]{:S(2)}) async-start(s32[4,1,128]{2,1,0:T(1,128)} %reshape.128), calls=%async_computation | async-start | bytes 4096 | tf_op jit(solution)/shard_map/all_to_all | solution.py:52
  17.5 1.4 scatter_custom_fusion.1
  18.9 2.6 %copy.16 = f32[8,16,1024]{1,0,2:T(8,128)} copy(f32[8,16,1024]{2,1,0:T(8,128)S(1)} %bitcast.33) | data formatting | bytes 1048576 | tf_op jit(solution)/shard_map/reshape | solution.py:14
  21.5 4.6 %reshape.130 = f32[4,1,32768]{2,1,0:T(1,128)} reshape(f32[1024,8,16]{2,1,0:T(8,128)} %bitcast.31) | data formatting | bytes 1048576
  26.1 5.1 %all-to-all-start.2 = ((f32[4,1,32768]{2,1,0:T(1,128)}), f32[4,1,32768]{2,1,0:T(1,128)S(1)}, u32[]{:S(2)}, u32[]{:S(2)}) async-start(f32[4,1,32768]{2,1,0:T(1,128)} %reshape.130), calls=%async_computation.2 | async-start | bytes 1048576 | tf_op jit(solution)/shard_map/all_to_all | solution.py:45
  31.2 0.5 broadcast.64
  31.7 0.7 reduce.4
  32.5 0.7 all_to_all.35
  33.1 12.0 %all-to-all-done.2 = f32[4,1,32768]{2,1,0:T(1,128)S(1)} async-done(((f32[4,1,32768]{2,1,0:T(1,128)}), f32[4,1,32768]{2,1,0:T(1,128)S(1)}, u32[]{:S(2)}, u32[]{:S(2)}) %all-to-all-start.2) | async-done | bytes 524320 | tf_op jit(solution)/shard_map/all_to_all | solution.py:45
  45.1 3.7 %all-to-all-start.1 = ((s32[8,64,1]{1,2,0:T(1,128)}), s32[8,64,1]{1,2,0:T(1,128)S(1)}, u32[]{:S(2)}, u32[]{:S(2)}) async-start(s32[8,64,1]{1,2,0:T(1,128)} %bitcast.5), calls=%async_computation.1 | async-start | bytes 8192 | tf_op jit(solution)/shard_map/all_to_all | solution.py:51
  49.3 2.1 %reduce.5 = f32[4,32768]{1,0:T(4,128)S(1)} reduce(f32[4,1,32768]{2,1,0:T(1,128)S(1)} %all-to-all-done.2, f32[]{:T(128)} %broadcast.65), dimensions={1}, to_apply=%all_to_all.37.reduce_sub_computation | reduce | bytes 1048580 | tf_op jit(solution)/shard_map/all_to_all | solution.py:45
  51.5 3.4 %reshape.131 = f32[1024,8,16]{2,1,0:T(8,128)} reshape(f32[4,32768]{1,0:T(4,128)S(1)} %reduce.5) | data formatting | bytes 1048576
  54.9 2.8 %copy.19 = f32[8,16,4,256]{3,2,1,0:T(4,128)S(1)} copy(f32[8,16,4,256]{1,0,3,2:T(8,128)} %bitcast.32) | data formatting | bytes 1048576 | tf_op jit(solution)/shard_map/all_to_all | solution.py:45
  57.8 0.9 copy.18
  58.7 4.2 %all-to-all-start.3 = ((f32[8,64,256]{2,1,0:T(8,128)}), f32[8,64,256]{2,1,0:T(8,128)S(1)}, u32[]{:S(2)}, u32[]{:S(2)}) async-start(f32[8,64,256]{2,1,0:T(8,128)} %bitcast.10), calls=%async_computation.3 | async-start | bytes 1048576 | tf_op jit(solution)/shard_map/all_to_all | solution.py:44
  63.0 0.5 broadcast.63
  63.5 0.7 reduce.3
  64.2 3.2 %scatter_custom_fusion.3 = f32[2048]{0:T(1024)S(1)} fusion(s32[512]{0:T(512)S(1)} %bitcast.39, f32[512]{0:T(512)S(1)} %broadcast.51, f32[]{:T(128)} %constant.8.clone.1), kind=kCustom, calls=%fused_computation.22 | custom fusion | flops 512 | bytes 8196 | tf_op jit(solution)/shard_map/scatter-add | solution.py:22
  67.5 5.1 %all-to-all-done.3 = f32[8,64,256]{2,1,0:T(8,128)S(1)} async-done(((f32[8,64,256]{2,1,0:T(8,128)}), f32[8,64,256]{2,1,0:T(8,128)S(1)}, u32[]{:S(2)}, u32[]{:S(2)}) %all-to-all-start.3) | async-done | bytes 524320 | tf_op jit(solution)/shard_map/all_to_all | solution.py:44
  72.6 4.0 %scatter_custom_fusion.2 = f32[2048,256]{1,0:T(8,128)S(1)} fusion(s32[512]{0:T(512)S(1)} %bitcast.40, f32[512,256]{1,0:T(8,128)S(1)} %bitcast.35, f32[]{:T(128)} %constant.8.clone.1), kind=kCustom, calls=%fused_computation.9 | custom fusion | flops 131072 | bytes 2097156 | tf_op jit(solution)/shard_map/scatter-add | solution.py:18
  76.6 2.9 %divide_add_fusion = f32[2048,256]{1,0:T(8,128)} fusion(f32[2048,256]{1,0:T(8,128)} %param.12, f32[2048,256]{1,0:T(8,128)S(1)} %scatter_custom_fusion.2, f32[2048]{0:T(1024)S(1)} %add.54, f32[2048]{0:T(1024)S(1)} %scatter_custom_fusion.3), kind=kLoop, calls=%fused_computation.8 | loop fusion | flops 2097152 | bytes 6307840 | tf_op jit(solution)/shard_map/add | solution.py:29
  79.5 14.1 %scatter_custom_fusion.4 = f32[4096,256]{1,0:T(8,128)} fusion(s32[2048]{0:T(1024)S(1)} %compare_select_fusion, f32[2048,256]{1,0:T(8,128)} %divide_add_fusion, f32[]{:T(128)} %constant.8.clone.1), kind=kCustom, calls=%fused_computation.6 | custom fusion | flops 524288 | bytes 4194816 | tf_op jit(solution)/shard_map/scatter-add | solution.py:18
  93.6 11.2 %scatter_custom_fusion.5 = f32[4096]{0:T(1024)S(1)} fusion(s32[2048]{0:T(1024)S(1)} %compare_select_fusion, f32[2048]{0:T(1024)S(1)} %broadcast.52, f32[]{:T(128)} %constant.8.clone.1), kind=kCustom, calls=%fused_computation.19 | custom fusion | flops 2048 | bytes 16388 | tf_op jit(solution)/shard_map/scatter-add | solution.py:22
  104.9 0.6 dynamic-slice
  106.2 23.2 %all-reduce = f32[4096]{0:T(1024)S(1)} all-reduce(f32[4096]{0:T(1024)S(1)} %scatter_custom_fusion.5), channel_id=3, replica_groups=mesh['rows'=4,'cx'=2,'cy'=4] {'cx','cy'}, use_global_device_ids=true, to_apply=%region_9.10.clone | all-reduce | flops 4096 | bytes 32768
  129.4 13.1 %reduce-scatter.2.cloned.1.call-done = f32[512,256]{1,0:T(8,128)} async-done(((f32[4096,256]{1,0:T(8,128)}), f32[512,256]{1,0:T(8,128)}) %reduce-scatter.2.cloned.1.call-update) | async-done | bytes 524304 | tf_op jit(solution)/shard_map/reduce_scatter | solution.py:68
  142.5 2.0 %divide_add_fusion.1 = f32[512,256]{1,0:T(8,128)} fusion(f32[512,256]{1,0:T(8,128)S(1)} %copy-done, f32[512,256]{1,0:T(8,128)} %reduce-scatter.2.cloned.1.call-done, f32[512]{0:T(512)S(1)} %get-tuple-element.4, f32[512]{0:T(512)S(1)} %get-tuple-element.5), kind=kLoop, calls=%fused_computation.11 | loop fusion | flops 524288 | bytes 1576960 | tf_op jit(solution)/shard_map/add | solution.py:29
  (35 shorter events, 1.1 us)
Async XLA Ops:
  11.2 14.9 %all-to-all-start = ((s32[4,1,128]{2,1,0:T(1,128)}), s32[4,1,128]{2,1,0:T(1,128)S(1)}, u32[]{:S(2)}, u32[]{:S(2)}) async-start(s32[4,1,128]{2,1,0:T(1,128)} %reshape.128), calls=%async_computation | async-start | bytes 4096 | tf_op jit(solution)/shard_map/all_to_all | solution.py:52
  26.1 19.0 %all-to-all-start.2 = ((f32[4,1,32768]{2,1,0:T(1,128)}), f32[4,1,32768]{2,1,0:T(1,128)S(1)}, u32[]{:S(2)}, u32[]{:S(2)}) async-start(f32[4,1,32768]{2,1,0:T(1,128)} %reshape.130), calls=%async_computation.2 | async-start | bytes 1048576 | tf_op jit(solution)/shard_map/all_to_all | solution.py:45
  45.1 13.5 %all-to-all-start.1 = ((s32[8,64,1]{1,2,0:T(1,128)}), s32[8,64,1]{1,2,0:T(1,128)S(1)}, u32[]{:S(2)}, u32[]{:S(2)}) async-start(s32[8,64,1]{1,2,0:T(1,128)} %bitcast.5), calls=%async_computation.1 | async-start | bytes 8192 | tf_op jit(solution)/shard_map/all_to_all | solution.py:51
  57.7 5.2 %copy-start.5 = (s32[2048,1]{0,1:T(1,128)S(1)}, s32[2048,1]{0,1:T(1,128)}, u32[]{:S(2)}) copy-start(s32[2048,1]{0,1:T(1,128)} %param.14) | copy-start | bytes 24580
  57.7 5.2 %copy-start.3 = (s32[2048]{0:T(1024)S(1)}, s32[2048]{0:T(1024)}, u32[]{:S(2)}) copy-start(s32[2048]{0:T(1024)} %param.15) | copy-start | bytes 24580
  57.8 9.7 %copy-start.4 = (f32[2048]{0:T(1024)S(1)}, f32[2048]{0:T(1024)}, u32[]{:S(2)}) copy-start(f32[2048]{0:T(1024)} %param.13) | copy-start | bytes 24580
  58.7 13.9 %all-to-all-start.3 = ((f32[8,64,256]{2,1,0:T(8,128)}), f32[8,64,256]{2,1,0:T(8,128)S(1)}, u32[]{:S(2)}, u32[]{:S(2)}) async-start(f32[8,64,256]{2,1,0:T(8,128)} %bitcast.10), calls=%async_computation.3 | async-start | bytes 1048576 | tf_op jit(solution)/shard_map/all_to_all | solution.py:44
  62.9 79.6 %reduce-scatter.2.cloned.1.call-start = ((), (), s32[]{:S(2)}) async-start(), calls=%async_computation.5 | async-start | bytes 4718592 | tf_op jit(solution)/shard_map/reduce_scatter | solution.py:68
  67.5 12.0 %copy-start.1 = (f32[2048]{0:T(1024)}, f32[2048]{0:T(1024)S(1)}, u32[]{:S(2)}) copy-start(f32[2048]{0:T(1024)S(1)} %add.54) | copy-start | bytes 24580
  93.6 11.3 %copy-start.7 = (u32[32]{0:T(128)S(1)}, u32[32]{0:T(128)}, u32[]{:S(2)}) copy-start(u32[32]{0:T(128)} %constant.5) | copy-start | bytes 388
  93.6 35.7 %copy-start.6 = (f32[512]{0:T(512)S(1)}, f32[512]{0:T(512)}, u32[]{:S(2)}) copy-start(f32[512]{0:T(512)} %param.17) | copy-start | bytes 6148
  93.6 48.9 %copy-start = (f32[512,256]{1,0:T(8,128)S(1)}, f32[512,256]{1,0:T(8,128)}, u32[]{:S(2)}) copy-start(f32[512,256]{1,0:T(8,128)} %param.16) | copy-start | bytes 1572868
  129.4 15.1 %copy-start.2 = (f32[512]{0:T(512)}, f32[512]{0:T(512)S(1)}, u32[]{:S(2)}) copy-start(f32[512]{0:T(512)S(1)} %get-tuple-element.4) | copy-start | bytes 6148
Sparse Core Ops, SparseCore 0:
  93.8 48.6 reduce-scatter.1
where the time goes:
time: 152 us; the launch traced here: 151 us
  other arithmetic  43.4 us (29%)
  waiting for transfers between devices  30.1 us (20%)
  blocking collectives  23.2 us (15%)
  local copies, waits for them, and re-layouts  20.4 us (13%)
  starting transfers between devices  19.4 us (13%)
  between operations  14.9 us (10%)
    unnamed x1, blocking collectives  23.2 us
    scatter-add x2, other arithmetic, accumulate(): jnp.zeros((segments, values.shape[1]), jnp.float32).at[labels]  18.1 us
    scatter-add x2, other arithmetic, accumulate(): member_counts = jnp.zeros((segments,), jnp.float32).at[labels].add(jnp.on...  14.5 us
    reduce_scatter x1, waiting for transfers between devices, body(): lax.psum_scatter(whole_partial, ('cx', 'cy'), scatter_dimension=0, tiled=...  13.1 us
    all_to_all x1, waiting for transfers between devices, body(): lax.all_to_all(buffer, 'rows', split_axis=2, concat_axis=1, tiled=True)  12 us
    unnamed x22, local copies, waits for them, and re-layouts  9.38 us
    all_to_all x1, starting transfers between devices, body(): lax.all_to_all(labels, 'rows', split_axis=2, concat_axis=1, tiled=True)  6.35 us
    all_to_all x1, starting transfers between devices, body(): lax.all_to_all(buffer, 'rows', split_axis=2, concat_axis=1, tiled=True)  5.09 us
  transfers between devices with their start and end apart: 5, of which 3 were waited for; matrix products, arithmetic and copies ran while one was open for 24% of the time, Pallas kernels for 0%

commit v1 on v0

--- a/solution.py
+++ b/solution.py
@@ -1,7 +1,15 @@
+import functools
+
 import jax
 import jax.numpy as jnp
 from jax import lax
+from jax.experimental import pallas as pl
+from jax.experimental.pallas import tpu as pltpu
 from jax.sharding import PartitionSpec as P
+
+MESH = pl.DeviceIdType.MESH
+LANES = 128
+CORES = 2
 
 
 def bucket(values, owners, slot_ids, shards, capacity, empty):
@@ -14,20 +22,252 @@
     return (buffer.reshape(shards, capacity, values.shape[1]), labels.reshape(shards, capacity))
 
 
-def accumulate(values, labels, segments):
-    summed = jnp.zeros((segments, values.shape[1]), jnp.float32).at[labels].add(values, mode="drop")
-    member_counts = (
-        jnp.zeros((segments,), jnp.float32)
-        .at[labels]
-        .add(jnp.ones(labels.shape, jnp.float32), mode="drop")
-    )
-    return (summed, member_counts)
-
-
-def damped(previous, weights, summed, member_counts):
-    denominator = weights + member_counts
-    updated = previous + (summed - member_counts[:, None] * previous) / denominator[:, None]
-    return (updated, denominator)
+def count_columns(ids_row, rows, base, limit):
+    spots = lax.broadcasted_iota(jnp.int32, (limit, LANES), 0) + base
+
+    def step(i, total):
+        line = jnp.broadcast_to(ids_row(i), (limit, LANES))
+        return total + jnp.where(line == spots, 1.0, 0.0)
+
+    total = lax.fori_loop(0, rows, step, jnp.zeros((limit, LANES), jnp.float32))
+    return jnp.sum(total, axis=1, keepdims=True)
+
+
+def local_kernel(lower_s, upper_s, lower_v, data, cent, counts, moved, news, partial, summed, members):
+    summed[...] = jnp.zeros_like(summed)
+    partial[...] = jnp.zeros_like(partial)
+
+    def add_row(i, _):
+        spot = lower_s[i]
+        summed[pl.ds(spot, 1), :] += data[pl.ds(i, 1), :]
+        return 0
+
+    lax.fori_loop(0, lower_s.shape[0], add_row, 0, unroll=8)
+    block = min(LANES, cent.shape[0])
+
+    def move(b, _):
+        here = pl.ds(pl.multiple_of(b * block, block), block)
+        m = count_columns(lambda i: lower_v[pl.ds(i, 1), :], lower_v.shape[0], b * block, block)
+        n = counts[here, :] + m
+        prev = cent[here, :]
+        moved[here, :] = prev + (summed[here, :] - m * prev) / n[:, :1]
+        news[here, :] = n
+        return 0
+
+    lax.fori_loop(0, cent.shape[0] // block, move, 0)
+
+    def add_moved(i, _):
+        spot = upper_s[i]
+        partial[pl.ds(spot, 1), :] += moved[pl.ds(i, 1), :]
+        return 0
+
+    lax.fori_loop(0, upper_s.shape[0], add_moved, 0, unroll=8)
+
+
+def local_update(labels, labels_upper, data, centroids, counts, slots):
+    rows, width = centroids.shape
+    vm = pl.BlockSpec(memory_space=pltpu.VMEM)
+    sm = pl.BlockSpec(memory_space=pltpu.SMEM)
+    return pl.pallas_call(
+        local_kernel,
+        out_shape=(
+            jax.ShapeDtypeStruct((rows, width), jnp.float32),
+            jax.ShapeDtypeStruct((rows, LANES), jnp.float32),
+            jax.ShapeDtypeStruct((slots, width), jnp.float32),
+        ),
+        in_specs=[sm, sm, vm, vm, vm, vm],
+        out_specs=(vm, vm, vm),
+        scratch_shapes=[
+            pltpu.VMEM((rows + 8, width), jnp.float32),
+            pltpu.VMEM((rows, LANES), jnp.float32),
+        ],
+        compiler_params=pltpu.CompilerParams(vmem_limit_bytes=60 * 1024 * 1024),
+        name="local_update",
+    )(
+        labels,
+        labels_upper,
+        labels.reshape(-1, LANES),
+        data,
+        centroids,
+        jnp.broadcast_to(counts[:, None], (rows, LANES)),
+    )
+
+
+def reduce_kernel(
+    ys, xs, part, ids, upper, weights, out, news,
+    pair, chip, a1, b1, a2, b2, seen,
+    s0, r0, sa1, ra1, sb1, rb1, sa2, ra2, sb2, rb2, si, ri,
+):
+    y = lax.axis_index("cx")
+    cy = lax.axis_index("cy")
+    x, core = lax.div(cy, CORES), lax.rem(cy, CORES)
+    cys = xs * CORES
+    shards = ys * cys
+    me = y * cys + cy
+    slots = part.shape[1]
+    half = slots // 2
+    lines = ids.shape[0]
+
+    barrier = pltpu.get_barrier_semaphore()
+    peers = []
+    for d in range(1, shards):
+        t = lax.rem(me + d, shards)
+        peers.append({"cx": lax.div(t, cys), "cy": lax.rem(t, cys)})
+    for peer in peers:
+        pl.semaphore_signal(barrier, inc=1, device_id=peer, device_id_type=MESH)
+    pl.semaphore_wait(barrier, shards - 1)
+
+    def remote(src, dst, send, recv, peer):
+        copy = pltpu.make_async_remote_copy(
+            src_ref=src, dst_ref=dst, send_sem=send, recv_sem=recv, device_id=peer, device_id_type=MESH
+        )
+        copy.start()
+        return copy
+
+    offsets = [(dy, dx) for dy in range(ys) for dx in range(xs)]
+    offsets.sort(key=lambda o: -((o[0] != 0) * 2 + (o[1] != 0) * 2))
+
+    def at(dy, dx):
+        return lax.rem(y + dy, ys), lax.rem(x + dx, xs)
+
+    started = []
+    first = {}
+    for dy, dx in offsets:
+        ty, tx = at(dy, dx)
+        k = dy * xs + dx
+        first[dy, dx] = remote(
+            part.at[(ty * xs + tx) * CORES + 1 - core], pair.at[k], s0.at[k], r0.at[k],
+            {"cx": y, "cy": x * CORES + 1 - core},
+        )
+    idc = [remote(ids, seen.at[d], si.at[d - 1], ri.at[d - 1], peers[d - 1]) for d in range(1, shards)]
+    seen[0] = ids[...]
+
+    ac, bc = {}, {}
+    for dy, dx in offsets:
+        ty, tx = at(dy, dx)
+        k = dy * xs + dx
+        first[dy, dx].wait_recv()
+        chip[k] = part[(ty * xs + tx) * CORES + core] + pair[k]
+        if dy:
+            ac[dy, dx] = remote(
+                chip.at[k, pl.ds(0, half)], a1.at[(dy - 1) * xs + dx],
+                sa1.at[(dy - 1) * xs + dx], ra1.at[(dy - 1) * xs + dx],
+                {"cx": ty, "cy": cy},
+            )
+        if dx:
+            bc[dy, dx] = remote(
+                chip.at[k, pl.ds(half, half)], b1.at[(dx - 1) * ys + dy],
+                sb1.at[(dx - 1) * ys + dy], rb1.at[(dx - 1) * ys + dy],
+                {"cx": y, "cy": tx * CORES + core},
+            )
+
+    a2c, b2c = {}, {}
+    for dx in range(1, xs):
+        for dy in range(1, ys):
+            ac[dy, dx].wait_recv()
+        total = chip[dx, :half]
+        for dy in range(1, ys):
+            total = total + a1[(dy - 1) * xs + dx]
+        chip[dx, :half] = total
+        a2c[dx] = remote(
+            chip.at[dx, pl.ds(0, half)], a2.at[dx - 1], sa2.at[dx - 1], ra2.at[dx - 1],
+            {"cx": y, "cy": lax.rem(x + dx, xs) * CORES + core},
+        )
+    for dy in range(1, ys):
+        for dx in range(1, xs):
+            bc[dy, dx].wait_recv()
+        total = chip[dy * xs, half:]
+        for dx in range(1, xs):
+            total = total + b1[(dx - 1) * ys + dy]
+        chip[dy * xs, half:] = total
+        b2c[dy] = remote(
+            chip.at[dy * xs, pl.ds(half, half)], b2.at[dy - 1], sb2.at[dy - 1], rb2.at[dy - 1],
+            {"cx": lax.rem(y + dy, ys), "cy": cy},
+        )
+
+    for copy in idc:
+        copy.wait_recv()
+    block = min(LANES, slots)
+    for b in range(slots // block):
+        here = pl.ds(b * block, block)
+        m = count_columns(
+            lambda i: seen[lax.div(i, lines), pl.ds(lax.rem(i, lines), 1), :],
+            shards * lines, me * slots + b * block, block,
+        )
+        n = weights[here, :] + m
+        news[here, :] = n
+        prev = upper[here, :]
+        out[here, :] = m * prev
+
+    for dy in range(1, ys):
+        ac[dy, 0].wait_recv()
+    for dx in range(1, xs):
+        bc[0, dx].wait_recv()
+    for dx in range(1, xs):
+        a2c[dx].wait_recv()
+    for dy in range(1, ys):
+        b2c[dy].wait_recv()
+
+    def close(rows, total):
+        prev = upper[rows, :]
+        out[rows, :] = prev + (total - out[rows, :]) / news[rows, :1]
+
+    total = chip[0, :half]
+    for dy in range(1, ys):
+        total = total + a1[(dy - 1) * xs]
+    for dx in range(1, xs):
+        total = total + a2[dx - 1]
+    close(pl.ds(0, half), total)
+    total = chip[0, half:]
+    for dx in range(1, xs):
+        total = total + b1[(dx - 1) * ys]
+    for dy in range(1, ys):
+        total = total + b2[dy - 1]
+    close(pl.ds(half, half), total)
+
+    for group in (first.values(), idc, ac.values(), bc.values(), a2c.values(), b2c.values()):
+        for copy in group:
+            copy.wait_send()
+
+
+def reduce_update(partial, ids, upper, weights, ys, xs):
+    slots, width = upper.shape
+    half = slots // 2
+    shards = ys * xs * CORES
+    vm = pl.BlockSpec(memory_space=pltpu.VMEM)
+    f32 = jnp.float32
+    n0, na, nb = ys * xs, (ys - 1) * xs, (xs - 1) * ys
+    dma = lambda n: pltpu.SemaphoreType.DMA((n,))
+    return pl.pallas_call(
+        functools.partial(reduce_kernel, ys, xs),
+        out_shape=(
+            jax.ShapeDtypeStruct((slots, width), f32),
+            jax.ShapeDtypeStruct((slots, LANES), f32),
+        ),
+        in_specs=[vm] * 4,
+        out_specs=(vm, vm),
+        scratch_shapes=[
+            pltpu.VMEM((n0, slots, width), f32),
+            pltpu.VMEM((n0, slots, width), f32),
+            pltpu.VMEM((na, half, width), f32),
+            pltpu.VMEM((nb, half, width), f32),
+            pltpu.VMEM((xs - 1, half, width), f32),
+            pltpu.VMEM((ys - 1, half, width), f32),
+            pltpu.VMEM((shards,) + ids.shape, jnp.int32),
+            dma(n0), dma(n0), dma(na), dma(na), dma(nb), dma(nb),
+            dma(xs - 1), dma(xs - 1), dma(ys - 1), dma(ys - 1),
+            dma(shards - 1), dma(shards - 1),
+        ],
+        compiler_params=pltpu.CompilerParams(
+            collective_id=1, has_side_effects=True, vmem_limit_bytes=60 * 1024 * 1024
+        ),
+        name="reduce_update",
+    )(
+        partial.reshape(shards, slots, width),
+        ids,
+        upper,
+        jnp.broadcast_to(weights[:, None], (slots, LANES)),
+    )
 
 
 def body(
@@ -57,20 +297,17 @@
         ),
     )
     slice_width = arrived.shape[2]
-    summed, member_counts = accumulate(
-        arrived.reshape(-1, slice_width), arrived_labels.reshape(-1), lower_rows
-    )
-    moved, new_counts = damped(centroids, counts, summed, member_counts)
     upper_rows = upper.shape[0]
-    owners_upper = owner_cent[:, 0]
-    labels_upper = owners_upper * upper_rows + slot_cent
-    whole_partial, hit_counts = accumulate(moved, labels_upper, upper_rows * shards)
-    upper_summed = lax.psum_scatter(whole_partial, ("cx", "cy"), scatter_dimension=0, tiled=True)
-    upper_members = lax.psum_scatter(hit_counts, ("cx", "cy"), scatter_dimension=0, tiled=True)
-    new_upper, new_upper_counts = damped(upper, upper_counts, upper_summed, upper_members)
-    return (moved, new_counts, new_upper, new_upper_counts)
-
-
+    ids = owner_cent[:, 0] * upper_rows + slot_cent
+    moved, news, partial = local_update(
+        arrived_labels.reshape(-1), ids, arrived.reshape(-1, slice_width), centroids, counts,
+        upper_rows * shards,
+    )
+    ys, xs = lax.axis_size("cx"), lax.axis_size("cy") // CORES
+    new_upper, new_weights = reduce_update(
+        partial, ids.reshape(-1, LANES), upper, upper_counts, ys, xs
+    )
+    return (moved, news[:, 0], new_upper, new_weights[:, 0])
 def solution(mesh):
     placed = (
         P(("rows", "cx", "cy"), None),

time: 152 us -> 121 us (0.80)
  Pallas kernels: 0 us -> 47.4 us
  other arithmetic: 43.4 us -> 6.4 us
  blocking collectives: 23.2 us -> 0 us
  between operations: 14.9 us -> 0.73 us
  waiting for transfers between devices: 30.1 us -> 18.6 us
  local copies, waits for them, and re-layouts: 20.4 us -> 27.7 us
    pallas_call x0 -> x2, Pallas kernels: none -> 47.4 us  [the longest x1 25.8 us: reduce_update(): pl.pallas_call(functools.partial(reduce_kernel, ys, xs), out_shape=(jax.S...]
    scatter-add x4 -> x0, other arithmetic: 32.6 us -> none  [the longest x2 18.1 us: accumulate(): jnp.zeros((segments, values.shape[1]), jnp.float32).at[labels]]
    unnamed x1 -> x0, blocking collectives: 23.2 us -> none
    reduce_scatter x1 -> x0, waiting for transfers between devices: 13.1 us -> none  [body(): lax.psum_scatter(whole_partial, ('cx', 'cy'), scatter_dimension=0, tiled=...]
    add x4 -> x1, other arithmetic: 5.03 us -> 0.6 us  [body(): ids = owner_cent[:, 0] * upper_rows + slot_cent]
    slice x0 -> x2, local copies, waits for them, and re-layouts: none -> 2.62 us  [body(): return (moved, news[:, 0], new_upper, new_weights[:, 0])]
    broadcast_in_dim x2, local copies, waits for them, and re-layouts: 0.01 us -> 2.19 us  [the longest x1 1.35 us: local_update(): jnp.broadcast_to(counts[:, None], (rows, LANES))]
    unnamed x22 -> x18, local copies, waits for them, and re-layouts: 9.38 us -> 10.6 us
  transfers between devices with their start and end apart: 5 -> 4, of which waited for: 3 -> 2; matrix products, arithmetic and copies ran while one was open for 24% -> 19% of each run, Pallas kernels for 0% -> 0%
where the time goes in v1:
time: 121 us; the launch traced here: 120 us
  Pallas kernels  47.4 us (39%)
  local copies, waits for them, and re-layouts  27.7 us (23%)
  starting transfers between devices  19.4 us (16%)
  waiting for transfers between devices  18.6 us (15%)
  other arithmetic  6.4 us (5%)
    pallas_call x1, Pallas kernels, reduce_update(): pl.pallas_call(functools.partial(reduce_kernel, ys, xs), out_shape=(jax.S...  25.8 us
    pallas_call x1, Pallas kernels, local_update(): pl.pallas_call(local_kernel, out_shape=(jax.ShapeDtypeStruct((rows, width...  21.5 us
    all_to_all x1, waiting for transfers between devices, body(): lax.all_to_all(buffer, 'rows', split_axis=2, concat_axis=1, tiled=True)  12 us
    unnamed x18, local copies, waits for them, and re-layouts  10.6 us
    all_to_all x1, waiting for transfers between devices, body(): lax.all_to_all(lax.all_to_all(buffer, 'rows', split_axis=2, concat_axis=1...  6.58 us
    all_to_all x1, starting transfers between devices, body(): lax.all_to_all(labels, 'rows', split_axis=2, concat_axis=1, tiled=True)  6.35 us
    all_to_all x1, starting transfers between devices, body(): lax.all_to_all(buffer, 'rows', split_axis=2, concat_axis=1, tiled=True)  5.09 us
    all_to_all x3, local copies, waits for them, and re-layouts, body(): lax.all_to_all(buffer, 'rows', split_axis=2, concat_axis=1, tiled=True)  4.28 us
  transfers between devices with their start and end apart: 4, of which 2 were waited for; matrix products, arithmetic and copies ran while one was open for 19% of the time, Pallas kernels for 0%

profile of v1, /device:TPU:0, one launch (start us, length us, event | category | flops | bytes accessed | tf_op | source)
XLA Modules:
  0.0 120.1 jit_solution(10109848436995088896)
XLA Ops:
  0.6 0.7 fusion.2
  1.5 0.8 select_reduce_fusion
  2.3 0.7 fusion.3
  3.0 0.9 scatter_custom_fusion
  4.0 0.7 reshape.68
  4.6 6.3 %all-to-all-start = ((s32[4,1,128]{2,1,0:T(1,128)}), s32[4,1,128]{2,1,0:T(1,128)S(1)}, u32[]{:S(2)}, u32[]{:S(2)}) async-start(s32[4,1,128]{2,1,0:T(1,128)} %reshape.68), calls=%async_computation | async-start | bytes 4096 | tf_op jit(solution)/shard_map/all_to_all | solution.py:292
  11.0 1.4 %scatter_custom_fusion.1 = f32[128,1024]{1,0:T(8,128)S(1)} fusion(s32[64]{0:T(128)S(1)} %fusion.3, f32[64,1024]{1,0:T(8,128)} %param.9, f32[]{:T(128)} %constant.16.clone.1), kind=kCustom, calls=%fused_computation.4 | custom fusion | bytes 524800 | tf_op jit(solution)/shard_map/scatter | solution.py:20
  12.3 2.6 %copy.19 = f32[8,16,1024]{1,0,2:T(8,128)} copy(f32[8,16,1024]{2,1,0:T(8,128)S(1)} %bitcast.33) | data formatting | bytes 1048576 | tf_op jit(solution)/shard_map/reshape | solution.py:22
  14.9 4.6 %reshape.70 = f32[4,1,32768]{2,1,0:T(1,128)} reshape(f32[1024,8,16]{2,1,0:T(8,128)} %bitcast.30) | data formatting | bytes 1048576
  19.6 5.1 %all-to-all-start.2 = ((f32[4,1,32768]{2,1,0:T(1,128)}), f32[4,1,32768]{2,1,0:T(1,128)S(1)}, u32[]{:S(2)}, u32[]{:S(2)}) async-start(f32[4,1,32768]{2,1,0:T(1,128)} %reshape.70), calls=%async_computation.2 | async-start | bytes 1048576 | tf_op jit(solution)/shard_map/all_to_all | solution.py:285
  24.6 0.5 broadcast.30
  25.2 0.7 reduce.10
  25.9 0.7 all_to_all.35
  26.6 12.0 %all-to-all-done.2 = f32[4,1,32768]{2,1,0:T(1,128)S(1)} async-done(((f32[4,1,32768]{2,1,0:T(1,128)}), f32[4,1,32768]{2,1,0:T(1,128)S(1)}, u32[]{:S(2)}, u32[]{:S(2)}) %all-to-all-start.2) | async-done | bytes 524320 | tf_op jit(solution)/shard_map/all_to_all | solution.py:285
  38.6 3.7 %all-to-all-start.1 = ((s32[8,64,1]{1,2,0:T(1,128)}), s32[8,64,1]{1,2,0:T(1,128)S(1)}, u32[]{:S(2)}, u32[]{:S(2)}) async-start(s32[8,64,1]{1,2,0:T(1,128)} %bitcast.5), calls=%async_computation.1 | async-start | bytes 8192 | tf_op jit(solution)/shard_map/all_to_all | solution.py:291
  42.8 2.1 %reduce.11 = f32[4,32768]{1,0:T(4,128)S(1)} reduce(f32[4,1,32768]{2,1,0:T(1,128)S(1)} %all-to-all-done.2, f32[]{:T(128)} %broadcast.31), dimensions={1}, to_apply=%all_to_all.37.reduce_sub_computation | reduce | bytes 1048580 | tf_op jit(solution)/shard_map/all_to_all | solution.py:285
  45.0 3.4 %reshape.71 = f32[1024,8,16]{2,1,0:T(8,128)} reshape(f32[4,32768]{1,0:T(4,128)S(1)} %reduce.11) | data formatting | bytes 1048576
  48.4 2.9 %copy.22 = f32[8,16,4,256]{3,2,1,0:T(4,128)S(1)} copy(f32[8,16,4,256]{1,0,3,2:T(8,128)} %bitcast.31) | data formatting | bytes 1048576 | tf_op jit(solution)/shard_map/all_to_all | solution.py:285
  51.3 0.9 copy.21
  52.1 4.2 %all-to-all-start.3 = ((f32[8,64,256]{2,1,0:T(8,128)}), f32[8,64,256]{2,1,0:T(8,128)S(1)}, u32[]{:S(2)}, u32[]{:S(2)}) async-start(f32[8,64,256]{2,1,0:T(8,128)} %bitcast.10), calls=%async_computation.3 | async-start | bytes 1048576 | tf_op jit(solution)/shard_map/all_to_all | solution.py:284
  56.4 0.6 add.14.upper_s
  57.5 0.7 reduce.9
  58.2 0.7 reshape.29.lower_s
  58.8 0.7 reshape_reshape.3.lower_v
  59.5 6.6 %all-to-all-done.3 = f32[8,64,256]{2,1,0:T(8,128)S(1)} async-done(((f32[8,64,256]{2,1,0:T(8,128)}), f32[8,64,256]{2,1,0:T(8,128)S(1)}, u32[]{:S(2)}, u32[]{:S(2)}) %all-to-all-start.3) | async-done | bytes 524320 | tf_op jit(solution)/shard_map/all_to_all | solution.py:284
  66.1 1.4 %broadcast_in_dim.32.counts = f32[2048,128]{1,0:T(8,128)} broadcast(f32[2048]{0:T(1024)S(1)} %copy-done.2), dimensions={0} | broadcast | bytes 1056768 | tf_op jit(solution)/shard_map/broadcast_in_dim | solution.py:92
  67.4 21.5 %local_update.1 = (f32[2048,256]{1,0:T(8,128)}, f32[2048,128]{1,0:T(8,128)}, f32[4096,256]{1,0:T(8,128)}) custom-call(s32[512]{0:T(512)} %reshape.29.lower_s, s32[2048]{0:T(1024)} %add.14.upper_s, s32[4,128]{1,0:T(4,128)} %reshape_reshape.3.lower_v, f32[512,256]{1,0:T(8,128)} %bitcast.35, f32[2048,256]{1,0:T(8,128)} %cent.1, f32[2048,128]{1,0:T(8,128)} %broadcast_in_dim.32.counts), custom_call_target="tpu_custom_call" | custom-call | tf_op jit(solution)/shard_map/local_update/pallas_call | solution.py:71
  89.0 0.8 broadcast_in_dim.33.weights
  89.8 25.8 %reduce_update.1 = (f32[512,256]{1,0:T(8,128)}, f32[512,128]{1,0:T(8,128)}) custom-call(f32[8,512,256]{2,1,0:T(8,128)} %bitcast.32, s32[16,128]{1,0:T(8,128)} %bitcast.36, f32[512,256]{1,0:T(8,128)} %upper.1, f32[512,128]{1,0:T(8,128)} %broadcast_in_dim.33.weights), custom_call_target="tpu_custom_call" | custom-call | tf_op jit(solution)/shard_map/reduce_update/pallas_call | solution.py:241
  115.6 1.7 %slice_reduce_fusion.1 = f32[512]{0:T(512)} fusion(f32[512,128]{1,0:T(8,128)} %get-tuple-element.13), kind=kLoop, calls=%fused_computation.3 | loop fusion | bytes 4096 | tf_op jit(solution)/shard_map/slice | solution.py:310
  117.3 0.9 slice_reduce_fusion
  118.2 1.9 %copy.24 = f32[512,256]{1,0:T(8,128)} copy(f32[512,256]{1,0:T(8,128)} %get-tuple-element.20) | data formatting | bytes 1048576
  (23 shorter events, 1.3 us)
Async XLA Ops:
  4.6 14.9 %all-to-all-start = ((s32[4,1,128]{2,1,0:T(1,128)}), s32[4,1,128]{2,1,0:T(1,128)S(1)}, u32[]{:S(2)}, u32[]{:S(2)}) async-start(s32[4,1,128]{2,1,0:T(1,128)} %reshape.68), calls=%async_computation | async-start | bytes 4096 | tf_op jit(solution)/shard_map/all_to_all | solution.py:292
  19.6 19.0 %all-to-all-start.2 = ((f32[4,1,32768]{2,1,0:T(1,128)}), f32[4,1,32768]{2,1,0:T(1,128)S(1)}, u32[]{:S(2)}, u32[]{:S(2)}) async-start(f32[4,1,32768]{2,1,0:T(1,128)} %reshape.70), calls=%async_computation.2 | async-start | bytes 1048576 | tf_op jit(solution)/shard_map/all_to_all | solution.py:285
  38.6 13.6 %all-to-all-start.1 = ((s32[8,64,1]{1,2,0:T(1,128)}), s32[8,64,1]{1,2,0:T(1,128)S(1)}, u32[]{:S(2)}, u32[]{:S(2)}) async-start(s32[8,64,1]{1,2,0:T(1,128)} %bitcast.5), calls=%async_computation.1 | async-start | bytes 8192 | tf_op jit(solution)/shard_map/all_to_all | solution.py:291
  48.4 8.0 %copy-start.4 = (s32[2048,1]{0,1:T(1,128)S(1)}, s32[2048,1]{0,1:T(1,128)}, u32[]{:S(2)}) copy-start(s32[2048,1]{0,1:T(1,128)} %param.14) | copy-start | bytes 24580
  48.4 8.0 %copy-start.3 = (s32[2048]{0:T(1024)S(1)}, s32[2048]{0:T(1024)}, u32[]{:S(2)}) copy-start(s32[2048]{0:T(1024)} %param.15) | copy-start | bytes 24580
  48.4 17.7 %copy-start.2 = (f32[2048]{0:T(1024)S(1)}, f32[2048]{0:T(1024)}, u32[]{:S(2)}) copy-start(f32[2048]{0:T(1024)} %param.13) | copy-start | bytes 24580
  51.2 37.7 %copy-start.5 = (f32[512]{0:T(512)S(1)}, f32[512]{0:T(512)}, u32[]{:S(2)}) copy-start(f32[512]{0:T(512)} %param.17) | copy-start | bytes 6148
  52.1 13.9 %all-to-all-start.3 = ((f32[8,64,256]{2,1,0:T(8,128)}), f32[8,64,256]{2,1,0:T(8,128)S(1)}, u32[]{:S(2)}, u32[]{:S(2)}) async-start(f32[8,64,256]{2,1,0:T(8,128)} %bitcast.10), calls=%async_computation.3 | async-start | bytes 1048576 | tf_op jit(solution)/shard_map/all_to_all | solution.py:284
  66.1 1.4 %copy-start = (f32[8,64,256]{2,1,0:T(8,128)}, f32[8,64,256]{2,1,0:T(8,128)S(1)}, u32[]{:S(2)}) copy-start(f32[8,64,256]{2,1,0:T(8,128)S(1)} %all-to-all-done.3) | copy-start | bytes 1572868
  89.0 28.3 %copy-start.1 = (f32[2048,128]{1,0:T(8,128)S(1)}, f32[2048,128]{1,0:T(8,128)}, u32[]{:S(2)}) copy-start(f32[2048,128]{1,0:T(8,128)} %get-tuple-element.10) | copy-start | bytes 3145732

commit v2 on v1

--- a/solution.py
+++ b/solution.py
@@ -12,14 +12,159 @@
 CORES = 2
 
 
-def bucket(values, owners, slot_ids, shards, capacity, empty):
-    onehot = (owners[:, None] == jnp.arange(shards, dtype=jnp.int32)[None, :]).astype(jnp.int32)
-    earlier = jnp.cumsum(onehot, axis=0) - onehot
-    position = jnp.sum(earlier * onehot, axis=1)
-    target = owners * capacity + position
-    buffer = jnp.zeros((shards * capacity, values.shape[1]), values.dtype).at[target].set(values)
-    labels = jnp.full((shards * capacity,), empty, jnp.int32).at[target].set(slot_ids)
-    return (buffer.reshape(shards, capacity, values.shape[1]), labels.reshape(shards, capacity))
+def exchange_kernel(
+    capacity, empty, rows_ref, owner_ref, slot_ref, data, labels,
+    info, mine, slabs, packed, inbox, tags, heard,
+    si, ri, ss, rs, sp, rp, st, rt,
+):
+    groups, batch, width = slabs.shape
+    shards = inbox.shape[0]
+    spots = shards * capacity
+    z = lax.axis_index("rows")
+    cys = lax.axis_size("cy")
+    me = lax.axis_index("cx") * cys + lax.axis_index("cy")
+
+    info[...] = jnp.full_like(info, -1)
+    info[0:1, :batch] = owner_ref[...]
+    info[1:2, :batch] = slot_ref[...]
+    tags[...] = jnp.full_like(tags, empty)
+
+    barrier = pltpu.get_barrier_semaphore()
+    mates = [{"rows": lax.rem(z + d, groups)} for d in range(1, groups)]
+    peers = []
+    for d in range(1, shards):
+        t = lax.rem(me + d, shards)
+        peers.append({"cx": lax.div(t, cys), "cy": lax.rem(t, cys)})
+    for peer in mates + peers:
+        pl.semaphore_signal(barrier, inc=1, device_id=peer, device_id_type=MESH)
+    pl.semaphore_wait(barrier, groups - 1 + shards - 1)
+
+    def remote(src, dst, send, recv, peer):
+        copy = pltpu.make_async_remote_copy(
+            src_ref=src, dst_ref=dst, send_sem=send, recv_sem=recv, device_id=peer, device_id_type=MESH
+        )
+        copy.start()
+        return copy
+
+    def columns(group):
+        return pl.ds(pl.multiple_of(group * width, width), width)
+
+    asked = [remote(info, mine.at[d], si.at[d - 1], ri.at[d - 1], mates[d - 1]) for d in range(1, groups)]
+    sent = [
+        remote(
+            rows_ref.at[:, columns(mates[d - 1]["rows"])], slabs.at[d],
+            ss.at[d - 1], rs.at[d - 1], mates[d - 1],
+        )
+        for d in range(1, groups)
+    ]
+    mine[0] = info[...]
+    slabs[0] = rows_ref[:, columns(z)]
+
+    bf16, f32 = jnp.bfloat16, jnp.float32
+    up = lax.broadcasted_iota(jnp.int32, (LANES, LANES), 0)
+    across = lax.broadcasted_iota(jnp.int32, (LANES, LANES), 1)
+    before = jnp.where(up < across, 1.0, 0.0).astype(bf16)
+    shard_of = lax.broadcasted_iota(jnp.int32, (shards, LANES), 0)
+    spot_of = lax.broadcasted_iota(jnp.int32, (spots, LANES), 0)
+    line = lax.broadcasted_iota(jnp.int32, (8, LANES), 0)
+    moves = []
+    for d in range(groups):
+        if d:
+            asked[d - 1].wait_recv()
+        owner, slot = mine[d, 0:1, :], mine[d, 1:2, :]
+        named = jnp.where(jnp.broadcast_to(owner, (shards, LANES)) == shard_of, 1.0, 0.0)
+        earlier = jnp.dot(named.astype(bf16), before, preferred_element_type=f32)
+        position = jnp.sum(named * earlier, axis=0, keepdims=True).astype(jnp.int32)
+        target = jnp.where(owner >= 0, owner * capacity + position, -1)
+        pick = jnp.where(jnp.broadcast_to(target, (spots, LANES)) == spot_of, 1.0, 0.0).astype(bf16)
+        high = jnp.broadcast_to(lax.shift_right_arithmetic(slot, 7), (8, LANES))
+        low = jnp.broadcast_to(slot & 127, (8, LANES))
+        code = jnp.where(line == 0, high, jnp.where(line == 1, low, 1)).astype(f32).astype(bf16)
+        found = lax.dot_general(code, pick, (((1,), (1,)), ((), ())), preferred_element_type=f32)
+        tag = (found[0:1] * 128.0 + found[1:2]).astype(jnp.int32)
+        tags[d : d + 1, :] = jnp.where(found[2:3] > 0.5, tag, empty)
+        if d:
+            sent[d - 1].wait_recv()
+        slab = slabs[d]
+        first = slab.astype(bf16)
+        left = slab - first.astype(f32)
+        second = left.astype(bf16)
+        third = (left - second.astype(f32)).astype(bf16)
+        chosen = pick[:, :batch]
+        total = jnp.dot(chosen, third, preferred_element_type=f32)
+        total = total + jnp.dot(chosen, second, preferred_element_type=f32)
+        packed[d] = total + jnp.dot(chosen, first, preferred_element_type=f32)
+        for p in range(1, shards):
+            t = lax.rem(me + p, shards)
+            k = (p - 1) * groups + d
+            moves.append(
+                remote(
+                    packed.at[d, pl.ds(pl.multiple_of(t * capacity, 8), capacity)], inbox.at[p, d],
+                    sp.at[k], rp.at[k], peers[p - 1],
+                )
+            )
+    told = [remote(tags, heard.at[p], st.at[p - 1], rt.at[p - 1], peers[p - 1]) for p in range(1, shards)]
+    heard[0] = tags[...]
+    for d in range(groups):
+        inbox[0, d] = packed[d, pl.ds(pl.multiple_of(me * capacity, 8), capacity), :]
+
+    per = LANES // capacity
+    lane = lax.broadcasted_iota(jnp.int32, (8, LANES), 1)
+    for copy in told:
+        copy.wait_recv()
+    for g in range(shards // per):
+        both = jnp.full((8, LANES), empty, jnp.int32)
+        for j in range(per):
+            p = g * per + j
+            turn = lax.rem((j + shards - me) * capacity, spots)
+            turned = pltpu.roll(heard[p], turn, 1)[:, :LANES]
+            both = jnp.where((lane >= j * capacity) & (lane < (j + 1) * capacity), turned, both)
+        labels[g * groups : (g + 1) * groups, :] = both[:groups]
+    for copy in moves:
+        copy.wait_recv()
+    for p in range(shards):
+        g, j = p // per, p % per
+        for d in range(groups):
+            data[pl.ds((g * groups + d) * LANES + j * capacity, capacity), :] = inbox[p, d]
+    for copy in asked + sent + moves + told:
+        copy.wait_send()
+
+
+def exchange(rows_data, owners, slot_rows, lower_rows, width):
+    shards = lax.axis_size(("cx", "cy"))
+    groups = lax.axis_size("rows")
+    batch = rows_data.shape[0]
+    capacity = -(-(2 * batch // shards) // 8) * 8
+    spots = shards * capacity
+    tall = -(-groups // 8) * 8
+    vm = pl.BlockSpec(memory_space=pltpu.VMEM)
+    f32, i32 = jnp.float32, jnp.int32
+    dma = lambda n: pltpu.SemaphoreType.DMA((n,))
+    many = (shards - 1) * groups
+    return pl.pallas_call(
+        functools.partial(exchange_kernel, capacity, lower_rows),
+        out_shape=(
+            jax.ShapeDtypeStruct((groups * spots, width), f32),
+            jax.ShapeDtypeStruct((groups * spots // LANES, LANES), i32),
+        ),
+        in_specs=[vm] * 3,
+        out_specs=(vm, vm),
+        scratch_shapes=[
+            pltpu.VMEM((8, LANES), i32),
+            pltpu.VMEM((groups, 8, LANES), i32),
+            pltpu.VMEM((groups, batch, width), f32),
+            pltpu.VMEM((groups, spots, width), f32),
+            pltpu.VMEM((shards, groups, capacity, width), f32),
+            pltpu.VMEM((tall, spots), i32),
+            pltpu.VMEM((shards, tall, spots), i32),
+            dma(groups - 1), dma(groups - 1), dma(groups - 1), dma(groups - 1),
+            dma(many), dma(many), dma(shards - 1), dma(shards - 1),
+        ],
+        compiler_params=pltpu.CompilerParams(
+            collective_id=2, has_side_effects=True, vmem_limit_bytes=60 * 1024 * 1024
+        ),
+        name="exchange",
+    )(rows_data, owners.reshape(1, batch), slot_rows.reshape(1, batch))
 
 
 def count_columns(ids_row, rows, base, limit):
@@ -33,69 +178,103 @@
     return jnp.sum(total, axis=1, keepdims=True)
 
 
-def local_kernel(lower_s, upper_s, lower_v, data, cent, counts, moved, news, partial, summed, members):
+def eye(size):
+    return lax.broadcasted_iota(jnp.int32, (size, size), 0) == lax.broadcasted_iota(jnp.int32, (size, size), 1)
+
+
+def to_column(row, same):
+    size = row.shape[1]
+    return jnp.sum(jnp.where(same, jnp.broadcast_to(row, (size, size)), 0.0), axis=1, keepdims=True)
+
+
+def to_row(column, same):
+    size = column.shape[0]
+    return jnp.sum(jnp.where(same, jnp.broadcast_to(column, (size, size)), 0.0), axis=0, keepdims=True)
+
+
+TOGETHER = 4
+
+
+def scatter_rows(table, source, count, label):
+    def step(i, _):
+        at = [i * TOGETHER + j for j in range(TOGETHER)]
+        place = [label(k) for k in at]
+        value = [source[pl.ds(k, 1), :] for k in at]
+        held = [table[pl.ds(p, 1), :] for p in place]
+        done = []
+        for j in range(TOGETHER):
+            total = held[j] + value[j]
+            for e in range(j):
+                total = total + jnp.where(place[e] == place[j], value[e], 0.0)
+            done.append(total)
+        for j in range(TOGETHER):
+            table[pl.ds(place[j], 1), :] = done[j]
+        return 0
+
+    lax.fori_loop(0, count // TOGETHER, step, 0, unroll=4)
+
+
+def local_kernel(lower_s, upper_s, lower_v, data, cent, counts, moved, news, partial, prev, now, summed, sems):
+    fetch = pltpu.make_async_copy(cent, prev, sems.at[0])
+    fetch.start()
     summed[...] = jnp.zeros_like(summed)
+    scatter_rows(
+        summed, data, data.shape[0],
+        lambda k: lower_s[lax.div(k, LANES), lax.rem(k, LANES)],
+    )
     partial[...] = jnp.zeros_like(partial)
-
-    def add_row(i, _):
-        spot = lower_s[i]
-        summed[pl.ds(spot, 1), :] += data[pl.ds(i, 1), :]
+    fetch.wait()
+    same = eye(LANES)
+
+    def move(b, _):
+        here = pl.ds(pl.multiple_of(b * LANES, LANES), LANES)
+        m = count_columns(lambda i: lower_v[pl.ds(i, 1), :], lower_v.shape[0], b * LANES, LANES)
+        n = to_column(counts[pl.ds(b, 1), :], same) + m
+        old = prev[here, :]
+        now[here, :] = old + (summed[here, :] - m * old) / n
+        news[pl.ds(b, 1), :] = to_row(n, same)
         return 0
 
-    lax.fori_loop(0, lower_s.shape[0], add_row, 0, unroll=8)
-    block = min(LANES, cent.shape[0])
-
-    def move(b, _):
-        here = pl.ds(pl.multiple_of(b * block, block), block)
-        m = count_columns(lambda i: lower_v[pl.ds(i, 1), :], lower_v.shape[0], b * block, block)
-        n = counts[here, :] + m
-        prev = cent[here, :]
-        moved[here, :] = prev + (summed[here, :] - m * prev) / n[:, :1]
-        news[here, :] = n
-        return 0
-
-    lax.fori_loop(0, cent.shape[0] // block, move, 0)
-
-    def add_moved(i, _):
-        spot = upper_s[i]
-        partial[pl.ds(spot, 1), :] += moved[pl.ds(i, 1), :]
-        return 0
-
-    lax.fori_loop(0, upper_s.shape[0], add_moved, 0, unroll=8)
-
-
-def local_update(labels, labels_upper, data, centroids, counts, slots):
+    lax.fori_loop(0, prev.shape[0] // LANES, move, 0)
+    put = pltpu.make_async_copy(now, moved, sems.at[1])
+    put.start()
+    scatter_rows(
+        partial, now, now.shape[0],
+        lambda k: upper_s[lax.div(k, LANES), lax.rem(k, LANES)],
+    )
+    put.wait()
+
+
+def local_update(labels, ids, data, centroids, counts, slots):
     rows, width = centroids.shape
     vm = pl.BlockSpec(memory_space=pltpu.VMEM)
     sm = pl.BlockSpec(memory_space=pltpu.SMEM)
-    return pl.pallas_call(
+    hbm = pl.BlockSpec(memory_space=pl.ANY)
+    f32 = jnp.float32
+    moved, news, partial = pl.pallas_call(
         local_kernel,
         out_shape=(
-            jax.ShapeDtypeStruct((rows, width), jnp.float32),
-            jax.ShapeDtypeStruct((rows, LANES), jnp.float32),
-            jax.ShapeDtypeStruct((slots, width), jnp.float32),
-        ),
-        in_specs=[sm, sm, vm, vm, vm, vm],
-        out_specs=(vm, vm, vm),
+            jax.ShapeDtypeStruct((rows, width), f32),
+            jax.ShapeDtypeStruct((rows // LANES, LANES), f32),
+            jax.ShapeDtypeStruct((slots, width), f32),
+        ),
+        in_specs=[sm, sm, vm, vm, hbm, vm],
+        out_specs=(hbm, vm, vm),
         scratch_shapes=[
-            pltpu.VMEM((rows + 8, width), jnp.float32),
-            pltpu.VMEM((rows, LANES), jnp.float32),
+            pltpu.VMEM((rows, width), f32),
+            pltpu.VMEM((rows, width), f32),
+            pltpu.VMEM((rows + 8, width), f32),
+            pltpu.SemaphoreType.DMA((2,)),
         ],
-        compiler_params=pltpu.CompilerParams(vmem_limit_bytes=60 * 1024 * 1024),
+        compiler_params=pltpu.CompilerParams(vmem_limit_bytes=40 * 1024 * 1024),
         name="local_update",
-    )(
-        labels,
-        labels_upper,
-        labels.reshape(-1, LANES),
-        data,
-        centroids,
-        jnp.broadcast_to(counts[:, None], (rows, LANES)),
-    )
+    )(labels, ids, labels, data, centroids, counts.reshape(-1, LANES))
+    return moved, news.reshape(-1), partial
 
 
 def reduce_kernel(
     ys, xs, part, ids, upper, weights, out, news,
-    pair, chip, a1, b1, a2, b2, seen,
+    pair, chip, a1, b1, a2, b2, seen, spread,
     s0, r0, sa1, ra1, sb1, rb1, sa2, ra2, sb2, rb2, si, ri,
 ):
     y = lax.axis_index("cx")
@@ -188,16 +367,17 @@
     for copy in idc:
         copy.wait_recv()
     block = min(LANES, slots)
+    same = eye(block)
     for b in range(slots // block):
         here = pl.ds(b * block, block)
         m = count_columns(
             lambda i: seen[lax.div(i, lines), pl.ds(lax.rem(i, lines), 1), :],
             shards * lines, me * slots + b * block, block,
         )
-        n = weights[here, :] + m
-        news[here, :] = n
-        prev = upper[here, :]
-        out[here, :] = m * prev
+        n = to_column(weights[b : b + 1, :], same) + m
+        news[b : b + 1, :] = to_row(n, same)
+        spread[here, :] = jnp.broadcast_to(n, (block, LANES))
+        out[here, :] = m * upper[here, :]
 
     for dy in range(1, ys):
         ac[dy, 0].wait_recv()
@@ -210,7 +390,7 @@
 
     def close(rows, total):
         prev = upper[rows, :]
-        out[rows, :] = prev + (total - out[rows, :]) / news[rows, :1]
+        out[rows, :] = prev + (total - out[rows, :]) / spread[rows, :1]
 
     total = chip[0, :half]
     for dy in range(1, ys):
@@ -233,16 +413,17 @@
 def reduce_update(partial, ids, upper, weights, ys, xs):
     slots, width = upper.shape
     half = slots // 2
+    block = min(LANES, slots)
     shards = ys * xs * CORES
     vm = pl.BlockSpec(memory_space=pltpu.VMEM)
     f32 = jnp.float32
     n0, na, nb = ys * xs, (ys - 1) * xs, (xs - 1) * ys
     dma = lambda n: pltpu.SemaphoreType.DMA((n,))
-    return pl.pallas_call(
+    new_upper, news = pl.pallas_call(
         functools.partial(reduce_kernel, ys, xs),
         out_shape=(
             jax.ShapeDtypeStruct((slots, width), f32),
-            jax.ShapeDtypeStruct((slots, LANES), f32),
+            jax.ShapeDtypeStruct((slots // block, block), f32),
         ),
         in_specs=[vm] * 4,
         out_specs=(vm, vm),
@@ -254,6 +435,7 @@
             pltpu.VMEM((xs - 1, half, width), f32),
             pltpu.VMEM((ys - 1, half, width), f32),
             pltpu.VMEM((shards,) + ids.shape, jnp.int32),
+            pltpu.VMEM((slots, LANES), f32),
             dma(n0), dma(n0), dma(na), dma(na), dma(nb), dma(nb),
             dma(xs - 1), dma(xs - 1), dma(ys - 1), dma(ys - 1),
             dma(shards - 1), dma(shards - 1),
@@ -266,48 +448,25 @@
         partial.reshape(shards, slots, width),
         ids,
         upper,
-        jnp.broadcast_to(weights[:, None], (slots, LANES)),
-    )
+        weights.reshape(-1, block),
+    )
+    return new_upper, news.reshape(-1)
 
 
 def body(
     rows_data, owner_rows, slot_rows, centroids, counts, owner_cent, slot_cent, upper, upper_counts
 ):
-    shards = lax.axis_size(("cx", "cy"))
-    groups = lax.axis_size("rows")
-    batch = rows_data.shape[0]
-    lower_rows = centroids.shape[0]
-    capacity = 2 * batch // shards
-    buffer, labels = bucket(rows_data, owner_rows[:, 0], slot_rows, shards, capacity, lower_rows)
-    labels = jnp.broadcast_to(labels[:, :, None], (shards, capacity, groups))
-    arrived, arrived_labels = (
-        lax.all_to_all(
-            lax.all_to_all(buffer, "rows", split_axis=2, concat_axis=1, tiled=True),
-            ("cx", "cy"),
-            split_axis=0,
-            concat_axis=0,
-            tiled=True,
-        ),
-        lax.all_to_all(
-            lax.all_to_all(labels, "rows", split_axis=2, concat_axis=1, tiled=True),
-            ("cx", "cy"),
-            split_axis=0,
-            concat_axis=0,
-            tiled=True,
-        ),
-    )
-    slice_width = arrived.shape[2]
+    ys, xs = lax.axis_size("cx"), lax.axis_size("cy") // CORES
     upper_rows = upper.shape[0]
-    ids = owner_cent[:, 0] * upper_rows + slot_cent
-    moved, news, partial = local_update(
-        arrived_labels.reshape(-1), ids, arrived.reshape(-1, slice_width), centroids, counts,
-        upper_rows * shards,
-    )
-    ys, xs = lax.axis_size("cx"), lax.axis_size("cy") // CORES
-    new_upper, new_weights = reduce_update(
-        partial, ids.reshape(-1, LANES), upper, upper_counts, ys, xs
-    )
-    return (moved, news[:, 0], new_upper, new_weights[:, 0])
+    ids = (owner_cent[:, 0] * upper_rows + slot_cent).reshape(-1, LANES)
+    data, labels = exchange(rows_data, owner_rows, slot_rows, *centroids.shape)
+    moved, new_counts, partial = local_update(
+        labels, ids, data, centroids, counts, upper_rows * ys * xs * CORES
+    )
+    new_upper, new_upper_counts = reduce_update(partial, ids, upper, upper_counts, ys, xs)
+    return (moved, new_counts, new_upper, new_upper_counts)
+
+
 def solution(mesh):
     placed = (
         P(("rows", "cx", "cy"), None),

time: 121 us -> 83.3 us (0.69)
  Pallas kernels: 47.4 us -> 71.7 us
  starting transfers between devices: 19.4 us -> 0 us
  local copies, waits for them, and re-layouts: 27.7 us -> 9.05 us
  waiting for transfers between devices: 18.6 us -> 0 us
  other arithmetic: 6.4 us -> 1.4 us
    pallas_call x0 -> x1, Pallas kernels: none -> 19.6 us  [exchange(): pl.pallas_call(functools.partial(exchange_kernel, capacity, lower_rows),...]
    all_to_all x4 -> x0, starting transfers between devices: 19.4 us -> none  [the longest x1 6.35 us: body(): lax.all_to_all(labels, 'rows', split_axis=2, concat_axis=1, tiled=True)]
    all_to_all x4 -> x0, waiting for transfers between devices: 18.6 us -> none  [the longest x1 12 us: body(): lax.all_to_all(buffer, 'rows', split_axis=2, concat_axis=1, tiled=True)]
    all_to_all x8 -> x0, local copies, waits for them, and re-layouts: 5.99 us -> none  [the longest x3 4.28 us: body(): lax.all_to_all(buffer, 'rows', split_axis=2, concat_axis=1, tiled=True)]
    pallas_call x1, Pallas kernels: 21.5 us -> 26.1 us  [local_update(): pl.pallas_call(local_kernel, out_shape=(jax.ShapeDtypeStruct((rows, width...]
    all_to_all x3 -> x0, other arithmetic: 3.46 us -> none  [the longest x1 2.14 us: body(): lax.all_to_all(buffer, 'rows', split_axis=2, concat_axis=1, tiled=True)]
    reshape x2 -> x0, local copies, waits for them, and re-layouts: 3.26 us -> none  [the longest x1 2.61 us: bucket(): buffer.reshape(shards, capacity, values.shape[1])]
    slice x2 -> x0, local copies, waits for them, and re-layouts: 2.62 us -> none  [body(): return (moved, news[:, 0], new_upper, new_weights[:, 0])]
  transfers between devices with their start and end apart: 4 -> 0, of which waited for: 2 -> 0; matrix products, arithmetic and copies ran while one was open for 19% -> 0% of each run, Pallas kernels for 0% -> 0%
where the time goes in v2:
time: 83.3 us; the launch traced here: 82.8 us
  Pallas kernels  71.7 us (86%)
  local copies, waits for them, and re-layouts  9.05 us (11%)
  other arithmetic  1.4 us (2%)
    pallas_call x1, Pallas kernels, local_update(): pl.pallas_call(local_kernel, out_shape=(jax.ShapeDtypeStruct((rows, width...  26.1 us
    pallas_call x1, Pallas kernels, reduce_update(): pl.pallas_call(functools.partial(reduce_kernel, ys, xs), out_shape=(jax.S...  25.9 us
    pallas_call x1, Pallas kernels, exchange(): pl.pallas_call(functools.partial(exchange_kernel, capacity, lower_rows),...  19.6 us
    unnamed x14, local copies, waits for them, and re-layouts  9.05 us

profile of v2, /device:TPU:0, one launch (start us, length us, event | category | flops | bytes accessed | tf_op | source)
XLA Modules:
  0.0 82.8 jit_solution(11680363095264328241)
XLA Ops:
  0.6 0.7 broadcast_multiply_fusion
  1.3 0.7 add_bitcast_fusion.upper_s.ids
  2.0 0.0 copy-start.3
  2.0 19.6 %exchange.1 = (f32[512,256]{1,0:T(8,128)}, s32[4,128]{1,0:T(4,128)}) custom-call(f32[64,1024]{1,0:T(8,128)} %rows_ref.1, s32[1,64]{1,0:T(1,128)} %bitcast.15, s32[1,64]{1,0:T(1,128)} %bitcast.16), custom_call_target="tpu_custom_call" | custom-call | tf_op jit(solution)/shard_map/exchange/pallas_call | solution.py:144
  21.7 0.0 copy-start.1
  21.7 1.6 %copy-done.1 = f32[2048,256]{1,0:T(8,128)S(1)} copy-done((f32[2048,256]{1,0:T(8,128)S(1)}, f32[2048,256]{1,0:T(8,128)}, u32[]{:S(2)}) %copy-start.1) | copy-done | bytes 2097176
  23.3 0.0 copy-start.2
  23.3 1.0 %copy-done.2 = f32[512,256]{1,0:T(8,128)S(1)} copy-done((f32[512,256]{1,0:T(8,128)S(1)}, f32[512,256]{1,0:T(8,128)}, u32[]{:S(2)}) %copy-start.2) | copy-done | bytes 524312
  24.3 0.0 copy-start.4
  24.3 0.7 copy-done.4
  25.0 0.0 copy-start.5
  25.0 0.7 copy-done.5
  25.7 26.1 %local_update.1 = (f32[2048,256]{1,0:T(8,128)}, f32[16,128]{1,0:T(8,128)}, f32[4096,256]{1,0:T(8,128)S(1)}) custom-call(s32[4,128]{1,0:T(4,128)S(1)} %copy-done.5, s32[16,128]{1,0:T(8,128)S(1)} %add_bitcast_fusion.upper_s.ids, s32[4,128]{1,0:T(4,128)S(1)} %copy-done.5, f32[512,256]{1,0:T(8,128)S(1)} %copy-done.2, f32[2048,256]{1,0:T(8,128)S(1)} %copy-done.1, ...), custom_call_target="tpu_custom_call" | custom-call | tf_op jit(solution)/shard_map/local_update/pallas_call | solution.py:254
  51.8 0.0 copy-start
  51.8 1.9 %copy-done = f32[4096,256]{1,0:T(8,128)} copy-done((f32[4096,256]{1,0:T(8,128)}, f32[4096,256]{1,0:T(8,128)S(1)}, u32[]{:S(2)}) %copy-start) | copy-done | bytes 4194328
  53.8 0.0 copy-done.3
  53.8 25.9 %reduce_update.1 = (f32[512,256]{1,0:T(8,128)}, f32[4,128]{1,0:T(4,128)}) custom-call(f32[8,512,256]{2,1,0:T(8,128)} %bitcast.10, s32[16,128]{1,0:T(8,128)} %copy-done.3, f32[512,256]{1,0:T(8,128)} %upper.1, f32[4,128]{1,0:T(4,128)} %bitcast.13), custom_call_target="tpu_custom_call" | custom-call | tf_op jit(solution)/shard_map/reduce_update/pallas_call | solution.py:422
  79.7 1.9 %copy.15 = f32[512,256]{1,0:T(8,128)} copy(f32[512,256]{1,0:T(8,128)} %get-tuple-element.24) | data formatting | bytes 1048576
  81.6 1.3 %copy.16 = f32[512]{0:T(512)} copy(f32[512]{0:T(512)} %bitcast.14) | data formatting | bytes 4096
Async XLA Ops:
  2.0 51.7 %copy-start.3 = (s32[16,128]{1,0:T(8,128)}, s32[16,128]{1,0:T(8,128)S(1)}, u32[]{:S(2)}) copy-start(s32[16,128]{1,0:T(8,128)S(1)} %add_bitcast_fusion.upper_s.ids) | copy-start | bytes 24580
  21.7 1.6 %copy-start.1 = (f32[2048,256]{1,0:T(8,128)S(1)}, f32[2048,256]{1,0:T(8,128)}, u32[]{:S(2)}) copy-start(f32[2048,256]{1,0:T(8,128)} %cent.1) | copy-start | bytes 6291460
  23.3 1.0 %copy-start.2 = (f32[512,256]{1,0:T(8,128)S(1)}, f32[512,256]{1,0:T(8,128)}, u32[]{:S(2)}) copy-start(f32[512,256]{1,0:T(8,128)} %get-tuple-element.12.data) | copy-start | bytes 1572868
  24.3 0.7 copy-start.4
  25.0 0.7 copy-start.5
  51.8 1.9 %copy-start = (f32[4096,256]{1,0:T(8,128)}, f32[4096,256]{1,0:T(8,128)S(1)}, u32[]{:S(2)}) copy-start(f32[4096,256]{1,0:T(8,128)S(1)} %get-tuple-element.15) | copy-start | bytes 12582916

commit v3 on v2

--- a/solution.py
+++ b/solution.py
@@ -161,7 +161,7 @@
             dma(many), dma(many), dma(shards - 1), dma(shards - 1),
         ],
         compiler_params=pltpu.CompilerParams(
-            collective_id=2, has_side_effects=True, vmem_limit_bytes=60 * 1024 * 1024
+            collective_id=2, has_side_effects=True, vmem_limit_bytes=16 * 1024 * 1024
         ),
         name="exchange",
     )(rows_data, owners.reshape(1, batch), slot_rows.reshape(1, batch))
@@ -192,56 +192,47 @@
     return jnp.sum(jnp.where(same, jnp.broadcast_to(column, (size, size)), 0.0), axis=0, keepdims=True)
 
 
-TOGETHER = 4
-
-
-def scatter_rows(table, source, count, label):
+def scatter_rows(tables, source, count, ids):
+    many = len(tables)
+    steps = LANES // many
+
     def step(i, _):
-        at = [i * TOGETHER + j for j in range(TOGETHER)]
-        place = [label(k) for k in at]
-        value = [source[pl.ds(k, 1), :] for k in at]
-        held = [table[pl.ds(p, 1), :] for p in place]
-        done = []
-        for j in range(TOGETHER):
-            total = held[j] + value[j]
-            for e in range(j):
-                total = total + jnp.where(place[e] == place[j], value[e], 0.0)
-            done.append(total)
-        for j in range(TOGETHER):
-            table[pl.ds(place[j], 1), :] = done[j]
+        line, first = lax.div(i, steps), lax.rem(i, steps) * many
+        for j, table in enumerate(tables):
+            table[pl.ds(ids[line, first + j], 1), :] += source[pl.ds(i * many + j, 1), :]
         return 0
 
-    lax.fori_loop(0, count // TOGETHER, step, 0, unroll=4)
-
-
-def local_kernel(lower_s, upper_s, lower_v, data, cent, counts, moved, news, partial, prev, now, summed, sems):
-    fetch = pltpu.make_async_copy(cent, prev, sems.at[0])
-    fetch.start()
-    summed[...] = jnp.zeros_like(summed)
-    scatter_rows(
-        summed, data, data.shape[0],
-        lambda k: lower_s[lax.div(k, LANES), lax.rem(k, LANES)],
-    )
-    partial[...] = jnp.zeros_like(partial)
-    fetch.wait()
+    lax.fori_loop(0, count // many, step, 0, unroll=8)
+
+
+def local_kernel(
+    lower_s, upper_s, lower_v, data, cent, counts, moved, news, partial, now, sum0, sum1, t1, t2, t3, sems
+):
+    for table in (sum0, sum1, partial, t1, t2, t3):
+        table[...] = jnp.zeros_like(table)
+    scatter_rows((sum0, sum1), data, data.shape[0], lower_s)
     same = eye(LANES)
 
     def move(b, _):
         here = pl.ds(pl.multiple_of(b * LANES, LANES), LANES)
         m = count_columns(lambda i: lower_v[pl.ds(i, 1), :], lower_v.shape[0], b * LANES, LANES)
         n = to_column(counts[pl.ds(b, 1), :], same) + m
-        old = prev[here, :]
-        now[here, :] = old + (summed[here, :] - m * old) / n
+        old = cent[here, :]
+        now[here, :] = old + (sum0[here, :] + sum1[here, :] - m * old) / n
         news[pl.ds(b, 1), :] = to_row(n, same)
         return 0
 
-    lax.fori_loop(0, prev.shape[0] // LANES, move, 0)
-    put = pltpu.make_async_copy(now, moved, sems.at[1])
+    lax.fori_loop(0, cent.shape[0] // LANES, move, 0)
+    put = pltpu.make_async_copy(now, moved, sems.at[0])
     put.start()
-    scatter_rows(
-        partial, now, now.shape[0],
-        lambda k: upper_s[lax.div(k, LANES), lax.rem(k, LANES)],
-    )
+    scatter_rows((partial, t1, t2, t3), now, now.shape[0], upper_s)
+
+    def join(b, _):
+        here = pl.ds(pl.multiple_of(b * LANES, LANES), LANES)
+        partial[here, :] = (partial[here, :] + t1[here, :]) + (t2[here, :] + t3[here, :])
+        return 0
+
+    lax.fori_loop(0, partial.shape[0] // LANES, join, 0)
     put.wait()
 
 
@@ -258,23 +249,26 @@
             jax.ShapeDtypeStruct((rows // LANES, LANES), f32),
             jax.ShapeDtypeStruct((slots, width), f32),
         ),
-        in_specs=[sm, sm, vm, vm, hbm, vm],
+        in_specs=[sm, sm, vm, vm, vm, vm],
         out_specs=(hbm, vm, vm),
         scratch_shapes=[
             pltpu.VMEM((rows, width), f32),
-            pltpu.VMEM((rows, width), f32),
             pltpu.VMEM((rows + 8, width), f32),
-            pltpu.SemaphoreType.DMA((2,)),
+            pltpu.VMEM((rows + 8, width), f32),
+            pltpu.VMEM((slots, width), f32),
+            pltpu.VMEM((slots, width), f32),
+            pltpu.VMEM((slots, width), f32),
+            pltpu.SemaphoreType.DMA((1,)),
         ],
-        compiler_params=pltpu.CompilerParams(vmem_limit_bytes=40 * 1024 * 1024),
+        compiler_params=pltpu.CompilerParams(vmem_limit_bytes=32 * 1024 * 1024),
         name="local_update",
     )(labels, ids, labels, data, centroids, counts.reshape(-1, LANES))
     return moved, news.reshape(-1), partial
 
 
 def reduce_kernel(
-    ys, xs, part, ids, upper, weights, out, news,
-    pair, chip, a1, b1, a2, b2, seen, spread,
+    ys, xs, part, ids, out, members,
+    pair, chip, a1, b1, a2, b2, seen,
     s0, r0, sa1, ra1, sb1, rb1, sa2, ra2, sb2, rb2, si, ri,
 ):
     y = lax.axis_index("cx")
@@ -367,17 +361,13 @@
     for copy in idc:
         copy.wait_recv()
     block = min(LANES, slots)
-    same = eye(block)
     for b in range(slots // block):
         here = pl.ds(b * block, block)
         m = count_columns(
             lambda i: seen[lax.div(i, lines), pl.ds(lax.rem(i, lines), 1), :],
             shards * lines, me * slots + b * block, block,
         )
-        n = to_column(weights[b : b + 1, :], same) + m
-        news[b : b + 1, :] = to_row(n, same)
-        spread[here, :] = jnp.broadcast_to(n, (block, LANES))
-        out[here, :] = m * upper[here, :]
+        members[here, :] = jnp.broadcast_to(m, (block, LANES))
 
     for dy in range(1, ys):
         ac[dy, 0].wait_recv()
@@ -388,26 +378,34 @@
     for dy in range(1, ys):
         b2c[dy].wait_recv()
 
-    def close(rows, total):
-        prev = upper[rows, :]
-        out[rows, :] = prev + (total - out[rows, :]) / spread[rows, :1]
-
     total = chip[0, :half]
     for dy in range(1, ys):
         total = total + a1[(dy - 1) * xs]
     for dx in range(1, xs):
         total = total + a2[dx - 1]
-    close(pl.ds(0, half), total)
+    out[:half, :] = total
     total = chip[0, half:]
     for dx in range(1, xs):
         total = total + b1[(dx - 1) * ys]
     for dy in range(1, ys):
         total = total + b2[dy - 1]
-    close(pl.ds(half, half), total)
+    out[half:, :] = total
 
     for group in (first.values(), idc, ac.values(), bc.values(), a2c.values(), b2c.values()):
         for copy in group:
             copy.wait_send()
+
+
+def finish_kernel(total, members, upper, weights, out, news):
+    lines, block = weights.shape
+    same = eye(block)
+    for b in range(lines):
+        here = pl.ds(b * block, block)
+        m = members[here, :1]
+        n = to_column(weights[b : b + 1, :], same) + m
+        prev = upper[here, :]
+        out[here, :] = prev + (total[here, :] - m * prev) / n
+        news[b : b + 1, :] = to_row(n, same)
 
 
 def reduce_update(partial, ids, upper, weights, ys, xs):
@@ -419,13 +417,13 @@
     f32 = jnp.float32
     n0, na, nb = ys * xs, (ys - 1) * xs, (xs - 1) * ys
     dma = lambda n: pltpu.SemaphoreType.DMA((n,))
-    new_upper, news = pl.pallas_call(
+    total, members = pl.pallas_call(
         functools.partial(reduce_kernel, ys, xs),
         out_shape=(
             jax.ShapeDtypeStruct((slots, width), f32),
-            jax.ShapeDtypeStruct((slots // block, block), f32),
-        ),
-        in_specs=[vm] * 4,
+            jax.ShapeDtypeStruct((slots, LANES), f32),
+        ),
+        in_specs=[vm] * 2,
         out_specs=(vm, vm),
         scratch_shapes=[
             pltpu.VMEM((n0, slots, width), f32),
@@ -435,21 +433,29 @@
             pltpu.VMEM((xs - 1, half, width), f32),
             pltpu.VMEM((ys - 1, half, width), f32),
             pltpu.VMEM((shards,) + ids.shape, jnp.int32),
-            pltpu.VMEM((slots, LANES), f32),
             dma(n0), dma(n0), dma(na), dma(na), dma(nb), dma(nb),
             dma(xs - 1), dma(xs - 1), dma(ys - 1), dma(ys - 1),
             dma(shards - 1), dma(shards - 1),
         ],
         compiler_params=pltpu.CompilerParams(
-            collective_id=1, has_side_effects=True, vmem_limit_bytes=60 * 1024 * 1024
+            collective_id=1, has_side_effects=True, vmem_limit_bytes=20 * 1024 * 1024
         ),
         name="reduce_update",
     )(
         partial.reshape(shards, slots, width),
         ids,
-        upper,
-        weights.reshape(-1, block),
     )
+    new_upper, news = pl.pallas_call(
+        finish_kernel,
+        out_shape=(
+            jax.ShapeDtypeStruct((slots, width), f32),
+            jax.ShapeDtypeStruct((slots // block, block), f32),
+        ),
+        in_specs=[vm] * 4,
+        out_specs=(vm, vm),
+        compiler_params=pltpu.CompilerParams(vmem_limit_bytes=8 * 1024 * 1024),
+        name="finish",
+    )(total, members, upper, weights.reshape(-1, block))
     return new_upper, news.reshape(-1)
 
 

time: 83.3 us -> 69.6 us (0.84)
  Pallas kernels: 71.7 us -> 62.6 us
  local copies, waits for them, and re-layouts: 9.05 us -> 4.55 us
    pallas_call x1, Pallas kernels: 26.1 us -> 20.9 us  [local_update(): pl.pallas_call(local_kernel, out_shape=(jax.ShapeDtypeStruct((rows, width...]
    unnamed x14, local copies, waits for them, and re-layouts: 9.05 us -> 4.55 us
    pallas_call x1, Pallas kernels: 25.9 us -> 22.7 us  [reduce_update(): pl.pallas_call(functools.partial(reduce_kernel, ys, xs), out_shape=(jax.S...]
    pallas_call x1, Pallas kernels: 19.6 us -> 17.9 us  [exchange(): pl.pallas_call(functools.partial(exchange_kernel, capacity, lower_rows),...]
    pallas_call x0 -> x1, Pallas kernels: none -> 1.11 us  [reduce_update(): pl.pallas_call(finish_kernel, out_shape=(jax.ShapeDtypeStruct((slots, wid...]
where the time goes in v3:
time: 69.6 us; the launch traced here: 69.3 us
  Pallas kernels  62.6 us (90%)
  local copies, waits for them, and re-layouts  4.55 us (7%)
  other arithmetic  1.4 us (2%)
  between operations  0.7 us (1%)
    pallas_call x1, Pallas kernels, reduce_update(): pl.pallas_call(functools.partial(reduce_kernel, ys, xs), out_shape=(jax.S...  22.7 us
    pallas_call x1, Pallas kernels, local_update(): pl.pallas_call(local_kernel, out_shape=(jax.ShapeDtypeStruct((rows, width...  20.9 us
    pallas_call x1, Pallas kernels, exchange(): pl.pallas_call(functools.partial(exchange_kernel, capacity, lower_rows),...  17.9 us
    unnamed x14, local copies, waits for them, and re-layouts  4.55 us

profile of v3, /device:TPU:0, one launch (start us, length us, event | category | flops | bytes accessed | tf_op | source)
XLA Modules:
  0.0 69.3 jit_solution(4421432982625457996)
XLA Ops:
  0.6 0.7 %broadcast_multiply_fusion = s32[2048,1]{0,1:T(1,128)S(1)} fusion(s32[2048,1]{0,1:T(1,128)} %param.14), kind=kLoop, calls=%fused_computation.1 | loop fusion | flops 2048 | bytes 16384 | tf_op jit(solution)/shard_map/mul | solution.py:467
  1.3 0.7 %add_bitcast_fusion.upper_s.ids = s32[16,128]{1,0:T(8,128)S(1)} fusion(s32[2048]{0:T(1024)S(1)} %bitcast.15, s32[2048]{0:T(1024)} %param.15), kind=kLoop, calls=%fused_computation | loop fusion | flops 2048 | bytes 24576 | tf_op jit(solution)/shard_map/reshape | solution.py:467
  2.0 0.0 copy-start.2
  2.0 0.9 %copy-done.2 = f32[64,1024]{1,0:T(8,128)S(1)} copy-done((f32[64,1024]{1,0:T(8,128)S(1)}, f32[64,1024]{1,0:T(8,128)}, u32[]{:S(2)}) %copy-start.2) | copy-done | bytes 262168
  3.0 0.0 copy-start.5
  3.0 0.7 copy-done.5
  3.6 0.0 copy-start.6
  3.6 0.7 copy-done.6
  4.3 17.9 %exchange.1 = (f32[512,256]{1,0:T(8,128)S(1)}, s32[4,128]{1,0:T(4,128)S(1)}) custom-call(f32[64,1024]{1,0:T(8,128)S(1)} %copy-done.2, s32[1,64]{1,0:T(1,128)S(1)} %bitcast.13, s32[1,64]{1,0:T(1,128)S(1)} %bitcast.14), custom_call_target="tpu_custom_call" | custom-call | tf_op jit(solution)/shard_map/exchange/pallas_call | solution.py:144
  22.2 0.0 copy-start
  22.2 1.6 %copy-done = f32[2048,256]{1,0:T(8,128)S(1)} copy-done((f32[2048,256]{1,0:T(8,128)S(1)}, f32[2048,256]{1,0:T(8,128)}, u32[]{:S(2)}) %copy-start) | copy-done | bytes 2097176
  23.8 0.0 copy-start.3
  23.8 0.7 %copy-done.3 = f32[2048]{0:T(1024)S(1)} copy-done((f32[2048]{0:T(1024)S(1)}, f32[2048]{0:T(1024)}, u32[]{:S(2)}) %copy-start.3) | copy-done | bytes 8216
  24.5 20.9 %local_update.1 = (f32[2048,256]{1,0:T(8,128)}, f32[16,128]{1,0:T(8,128)}, f32[4096,256]{1,0:T(8,128)S(1)}) custom-call(s32[4,128]{1,0:T(4,128)S(1)} %get-tuple-element.13.lower_s.lower_v, s32[16,128]{1,0:T(8,128)S(1)} %add_bitcast_fusion.upper_s.ids, s32[4,128]{1,0:T(4,128)S(1)} %get-tuple-element.13.lower_s.lower_v, ...), custom_call_target="tpu_custom_call" | custom-call | tf_op jit(solution)/shard_map/local_update/pallas_call | solution.py:245
  45.4 0.0 copy-start.1
  45.4 0.0 copy-start.4
  45.4 22.7 %reduce_update.1 = (f32[512,256]{1,0:T(8,128)S(1)}, f32[512,128]{1,0:T(8,128)S(1)}) custom-call(f32[8,512,256]{2,1,0:T(8,128)S(1)} %bitcast.10, s32[16,128]{1,0:T(8,128)S(1)} %add_bitcast_fusion.upper_s.ids), custom_call_target="tpu_custom_call" | custom-call | tf_op jit(solution)/shard_map/reduce_update/pallas_call | solution.py:420
  68.2 0.0 copy-done.1
  68.2 0.0 copy-done.4
  68.2 1.1 %finish.1 = (f32[512,256]{1,0:T(8,128)}, f32[4,128]{1,0:T(4,128)}) custom-call(f32[512,256]{1,0:T(8,128)S(1)} %get-tuple-element.18.total, f32[512,128]{1,0:T(8,128)S(1)} %get-tuple-element.19.members, f32[512,256]{1,0:T(8,128)S(1)} %copy-done.1, f32[4,128]{1,0:T(4,128)S(1)} %bitcast.12), custom_call_target="tpu_custom_call" | custom-call | tf_op jit(solution)/shard_map/finish/pallas_call | solution.py:448
Async XLA Ops:
  2.0 0.9 %copy-start.2 = (f32[64,1024]{1,0:T(8,128)S(1)}, f32[64,1024]{1,0:T(8,128)}, u32[]{:S(2)}) copy-start(f32[64,1024]{1,0:T(8,128)} %rows_ref.1) | copy-start | bytes 786436
  3.0 0.7 copy-start.5
  3.6 0.7 copy-start.6
  22.2 1.6 %copy-start = (f32[2048,256]{1,0:T(8,128)S(1)}, f32[2048,256]{1,0:T(8,128)}, u32[]{:S(2)}) copy-start(f32[2048,256]{1,0:T(8,128)} %cent.1) | copy-start | bytes 6291460
  23.8 0.7 %copy-start.3 = (f32[2048]{0:T(1024)S(1)}, f32[2048]{0:T(1024)}, u32[]{:S(2)}) copy-start(f32[2048]{0:T(1024)} %param.13) | copy-start | bytes 24580
  45.4 22.7 %copy-start.1 = (f32[512,256]{1,0:T(8,128)S(1)}, f32[512,256]{1,0:T(8,128)}, u32[]{:S(2)}) copy-start(f32[512,256]{1,0:T(8,128)} %upper.1) | copy-start | bytes 1572868
  45.4 22.7 %copy-start.4 = (f32[512]{0:T(512)S(1)}, f32[512]{0:T(512)}, u32[]{:S(2)}) copy-start(f32[512]{0:T(512)} %param.17) | copy-start | bytes 6148
